TPU v7x, 256 devices: a whole 4x4x8 slice. The times are simulated.
256 devices in a mesh: owner: 8 (over x, core), rows: 32 (over z, y).
Axes of the slice: x: 4, y: 4, z: 8, core: 2. Of those that a mesh axis runs over, the one named last changes fastest.
Arguments:
- w_down: float32 [16, 6400, 4096], P('owner', None, 'rows'), may hold values from -0.15625 to 0.15625
- avg_down: bfloat16 [16, 6400, 4096], P('owner', None, 'rows'), may hold values from -0.0390625 to 0.0390625
- router_weight: float32 [4096, 16], P('rows', 'owner'), may hold values from -0.09375 to 0.09375
- router_gain: float32 [4096], P('rows'), may hold values from 0.25 to 1.75
Outputs:
- serve_down: bfloat16 [16, 6400, 4096], P('owner', 'rows')
- scale_down: float32 [16, 6400], P('owner', 'rows')
- serve_router: bfloat16 [4096, 16], replicated
All inputs are finite; a program needn't handle non-finite values. Where the computation divides by a largest or mean magnitude, that divisor is 1e-20 or more.
Results may differ from a plain program's by a relative error of at most 0.001.
Values may be sent and summed in bfloat16 or wider, within the bound.
A program may use at most 64 MiB of HBM per device.

v0:
```python
import jax
import jax.numpy as jnp
from jax import lax
from jax.sharding import PartitionSpec as P

D_MODEL = 4096


def copy_for_each(x, axis):
    count = lax.axis_size(axis)
    return lax.all_to_all(jnp.broadcast_to(x[None], (count, *x.shape)), axis, 0, 0, tiled=True)


def over_copies(x, axis):
    everything = copy_for_each(x, axis)
    return jnp.sum(everything, axis=0)


def laid_out(parts, dim):
    shape = list(parts.shape[1:])
    shape[dim] *= parts.shape[0]
    return jnp.moveaxis(parts, 0, dim).reshape(shape)


def collect(x, axis, dim):
    return laid_out(copy_for_each(x, axis), dim)


def per_device(w_down, avg_down, router_weight, router_gain):
    fresh_down = w_down + avg_down.astype(jnp.float32)
    total_down = over_copies(jnp.sum(jnp.abs(fresh_down), axis=2), "rows")
    scale_down = total_down / D_MODEL
    narrow_down = (fresh_down / jnp.expand_dims(scale_down, 2)).astype(jnp.bfloat16)
    serve_down = lax.all_to_all(narrow_down, "rows", split_axis=1, concat_axis=2, tiled=True)
    scale_down = lax.dynamic_slice_in_dim(
        scale_down, lax.axis_index("rows") * serve_down.shape[1], serve_down.shape[1], axis=1
    )
    part_router = (router_weight * router_gain[:, None]).astype(jnp.bfloat16)
    row_router = collect(part_router, "rows", 0)
    serve_router = collect(row_router, "owner", 1)
    return (serve_down, scale_down, serve_router)


def solution(mesh):
    return jax.shard_map(
        per_device,
        mesh=mesh,
        in_specs=(
            P("owner", None, "rows"),
            P("owner", None, "rows"),
            P("rows", "owner"),
            P("rows"),
        ),
        out_specs=(P("owner", "rows", None), P("owner", "rows"), P()),
        check_vma=False,
    )
```

profile of v0, /device:TPU:9, one launch (start us, length us, event | category | flops | bytes accessed | tf_op | source)
XLA Modules:
  0.0 201.1 jit_solution(2779808520759683975)
XLA Ops:
  0.6 0.7 multiply_convert_fusion
  1.3 0.6 broadcast_in_dim.9
  1.9 11.1 %all-to-all-start.2 = ((bf16[32,128,2]{1,2,0:T(2,128)(2,1)}), bf16[32,128,2]{1,2,0:T(2,128)(2,1)S(1)}, u32[]{:S(2)}, u32[]{:S(2)}) async-start(bf16[32,128,2]{1,2,0:T(2,128)(2,1)} %broadcast_in_dim.9), calls=%async_computation.2 | async-start | bytes 32768 | tf_op jit(solution)/shard_map/all_to_all | solution.py:11
  13.1 5.6 %abs_reduce_fusion = f32[2,6400]{1,0:T(2,128)S(1)} fusion(f32[2,6400,128]{2,1,0:T(8,128)} %param.4, bf16[2,6400,128]{2,1,0:T(8,128)(2,1)} %param.5), kind=kLoop, calls=%fused_computation.1 | loop fusion | flops 6540800 | bytes 9881600 | tf_op jit(solution)/shard_map/reduce_sum | solution.py:31
  18.7 0.0 copy-start
  18.7 2.0 all-to-all-done.2
  20.7 0.4 broadcast_in_dim.8
  21.1 46.8 %all_to_all.33 = f32[32,2,6400]{2,1,0:T(2,128)} all-to-all(f32[32,2,6400]{2,1,0:T(2,128)S(1)} %broadcast_in_dim.8), channel_id=1, replica_groups=mesh['owner'=8,'rows'=32] {'rows'}, dimensions={0} | all-to-all | bytes 3276800 | tf_op jit(solution)/shard_map/all_to_all | solution.py:11
  67.9 0.7 broadcast_in_dim.11
  68.6 6.7 %all-to-all-start.3 = ((bf16[8,4096,2]{1,2,0:T(2,128)(2,1)}), bf16[8,4096,2]{1,2,0:T(2,128)(2,1)S(1)}, u32[]{:S(2)}, u32[]{:S(2)}) async-start(bf16[8,4096,2]{1,2,0:T(2,128)(2,1)} %broadcast_in_dim.11), calls=%async_computation.3 | async-start | bytes 262144 | tf_op jit(solution)/shard_map/all_to_all | solution.py:11
  75.4 1.9 reduce_sum.19
  77.3 0.0 copy-done
  77.3 4.7 %divide_convert_fusion = bf16[2,6400,128]{2,1,0:T(8,128)(2,1)S(1)} fusion(f32[2,6400,128]{2,1,0:T(8,128)} %param.4, bf16[2,6400,128]{2,1,0:T(8,128)(2,1)S(1)} %copy-done, f32[2,6400]{1,0:T(2,128)S(1)} %broadcast_multiply_fusion), kind=kLoop, calls=%fused_computation | loop fusion | flops 6553600 | bytes 13158400 | tf_op jit(solution)/shard_map/convert_element_type | solution.py:33
  82.0 27.9 %copy.31 = bf16[2,6400,128]{2,0,1:T(2,128)(2,1)} copy(bf16[2,6400,128]{2,1,0:T(8,128)(2,1)S(1)} %divide_convert_fusion) | data formatting | bytes 6553600 | tf_op jit(solution)/shard_map/convert_element_type | solution.py:33
  109.9 0.0 all-to-all-done.3
  109.9 5.0 %all-to-all-start.1 = ((bf16[2,6400,128]{2,0,1:T(2,128)(2,1)}), bf16[2,6400,128]{2,0,1:T(2,128)(2,1)S(1)}, u32[]{:S(2)}, u32[]{:S(2)}) async-start(bf16[2,6400,128]{2,0,1:T(2,128)(2,1)} %copy.31), calls=%async_computation.1 | async-start | bytes 6553600 | tf_op jit(solution)/shard_map/all_to_all | solution.py:34
  114.9 0.7 reshape.16
  115.7 0.7 constant_dynamic-slice_fusion
  116.3 76.1 %all-to-all-done.1 = bf16[2,6400,128]{2,0,1:T(2,128)(2,1)S(1)} async-done(((bf16[2,6400,128]{2,0,1:T(2,128)(2,1)}), bf16[2,6400,128]{2,0,1:T(2,128)(2,1)S(1)}, u32[]{:S(2)}, u32[]{:S(2)}) %all-to-all-start.1) | async-done | bytes 3276832 | tf_op jit(solution)/shard_map/all_to_all | solution.py:34
  192.4 2.5 %copy.32 = bf16[2,200,32,128]{3,2,1,0:T(8,128)(2,1)} copy(bf16[2,200,32,128]{3,0,1,2:T(2,128)(2,1)S(1)} %bitcast.9) | data formatting | bytes 6553600 | tf_op jit(solution)/shard_map/all_to_all | solution.py:34
  194.9 6.2 %all_to_all.26 = bf16[2,200,4096]{2,1,0:T(8,128)(2,1)} reshape(bf16[2,200,32,128]{3,2,1,0:T(8,128)(2,1)} %copy.32) | data formatting | bytes 6553600 | tf_op jit(solution)/shard_map/all_to_all | solution.py:34
  (1 shorter events, 0.0 us)
Async XLA Ops:
  1.9 18.8 %all-to-all-start.2 = ((bf16[32,128,2]{1,2,0:T(2,128)(2,1)}), bf16[32,128,2]{1,2,0:T(2,128)(2,1)S(1)}, u32[]{:S(2)}, u32[]{:S(2)}) async-start(bf16[32,128,2]{1,2,0:T(2,128)(2,1)} %broadcast_in_dim.9), calls=%async_computation.2 | async-start | bytes 32768 | tf_op jit(solution)/shard_map/all_to_all | solution.py:11
  18.7 58.6 %copy-start = (bf16[2,6400,128]{2,1,0:T(8,128)(2,1)S(1)}, bf16[2,6400,128]{2,1,0:T(8,128)(2,1)}, u32[]{:S(2)}) copy-start(bf16[2,6400,128]{2,1,0:T(8,128)(2,1)} %param.5) | copy-start | bytes 9830404
  68.6 41.3 %all-to-all-start.3 = ((bf16[8,4096,2]{1,2,0:T(2,128)(2,1)}), bf16[8,4096,2]{1,2,0:T(2,128)(2,1)S(1)}, u32[]{:S(2)}, u32[]{:S(2)}) async-start(bf16[8,4096,2]{1,2,0:T(2,128)(2,1)} %broadcast_in_dim.11), calls=%async_computation.3 | async-start | bytes 262144 | tf_op jit(solution)/shard_map/all_to_all | solution.py:11
  109.9 82.5 %all-to-all-start.1 = ((bf16[2,6400,128]{2,0,1:T(2,128)(2,1)}), bf16[2,6400,128]{2,0,1:T(2,128)(2,1)S(1)}, u32[]{:S(2)}, u32[]{:S(2)}) async-start(bf16[2,6400,128]{2,0,1:T(2,128)(2,1)} %copy.31), calls=%async_computation.1 | async-start | bytes 6553600 | tf_op jit(solution)/shard_map/all_to_all | solution.py:34
where the time goes:
time: 202 us; the launch traced here: 201 us
  waiting for transfers between devices  78.1 us (39%)
  blocking collectives  46.8 us (23%)
  local copies, waits for them, and re-layouts  39.7 us (20%)
  starting transfers between devices  22.9 us (11%)
  other arithmetic  12.9 us (6%)
    all_to_all x1, waiting for transfers between devices, per_device(): lax.all_to_all(narrow_down, 'rows', split_axis=1, concat_axis=2, tiled=True)  76.1 us
    all_to_all x1, blocking collectives, copy_for_each(): lax.all_to_all(jnp.broadcast_to(x[None], (count, *x.shape)), axis, 0, 0,...  46.8 us
    convert_element_type x1, local copies, waits for them, and re-layouts, per_device(): (fresh_down / jnp.expand_dims(scale_down, 2)).astype(jnp.bfloat16)  27.9 us
    all_to_all x2, starting transfers between devices, copy_for_each(): lax.all_to_all(jnp.broadcast_to(x[None], (count, *x.shape)), axis, 0, 0,...  17.8 us
    all_to_all x2, local copies, waits for them, and re-layouts, per_device(): lax.all_to_all(narrow_down, 'rows', split_axis=1, concat_axis=2, tiled=True)  8.72 us
    reduce_sum x1, other arithmetic, per_device(): total_down = over_copies(jnp.sum(jnp.abs(fresh_down), axis=2), 'rows')  5.6 us
    all_to_all x1, starting transfers between devices, per_device(): lax.all_to_all(narrow_down, 'rows', split_axis=1, concat_axis=2, tiled=True)  5.01 us
    convert_element_type x1, other arithmetic, per_device(): (fresh_down / jnp.expand_dims(scale_down, 2)).astype(jnp.bfloat16)  4.74 us
  transfers between devices with their start and end apart: 3, of which 2 were waited for; matrix products, arithmetic and copies ran while one was open for 21% of the time, Pallas kernels for 0%

commit v1 on v0

--- a/solution.py
+++ b/solution.py
@@ -4,6 +4,15 @@
 from jax.sharding import PartitionSpec as P
 
 D_MODEL = 4096
+_apply_task = lambda q_in, axis_tag, array_axis, dimension_no: jnp.concatenate(
+    lax.all_to_all(
+        jnp.stack(jnp.split(q_in, lax.axis_size(axis_tag), axis=array_axis), axis=0),
+        axis_name=axis_tag,
+        split_axis=0,
+        concat_axis=0,
+    ),
+    axis=dimension_no,
+)
 
 
 def copy_for_each(x, axis):
@@ -31,7 +40,7 @@
     total_down = over_copies(jnp.sum(jnp.abs(fresh_down), axis=2), "rows")
     scale_down = total_down / D_MODEL
     narrow_down = (fresh_down / jnp.expand_dims(scale_down, 2)).astype(jnp.bfloat16)
-    serve_down = lax.all_to_all(narrow_down, "rows", split_axis=1, concat_axis=2, tiled=True)
+    serve_down = _apply_task(narrow_down, "rows", 1, 2)
     scale_down = lax.dynamic_slice_in_dim(
         scale_down, lax.axis_index("rows") * serve_down.shape[1], serve_down.shape[1], axis=1
     )

time: 202 us -> 170 us (0.84)
  local copies, waits for them, and re-layouts: 39.7 us -> 7.53 us
    convert_element_type x1 -> x0, local copies, waits for them, and re-layouts: 27.9 us -> none  [per_device(): (fresh_down / jnp.expand_dims(scale_down, 2)).astype(jnp.bfloat16)]
    all_to_all x2 -> x0, local copies, waits for them, and re-layouts: 8.72 us -> none  [per_device(): lax.all_to_all(narrow_down, 'rows', split_axis=1, concat_axis=2, tiled=True)]
    unnamed x2 -> x35, local copies, waits for them, and re-layouts: 0.01 us -> 2.25 us
    reshape x0 -> x1, local copies, waits for them, and re-layouts: none -> 2.14 us  [jnp.concatenate(lax.all_to_all(jnp.stack(jnp.split(q_in, lax.axis_size(ax...]
  transfers between devices with their start and end apart: 3 -> 3, of which waited for: 2 -> 2; matrix products, arithmetic and copies ran while one was open for 21% -> 8% of each run, Pallas kernels for 0% -> 0%
where the time goes in v1:
time: 170 us; the launch traced here: 169 us
  waiting for transfers between devices  78.1 us (46%)
  blocking collectives  46.8 us (28%)
  starting transfers between devices  22.9 us (13%)
  other arithmetic  12.9 us (8%)
  local copies, waits for them, and re-layouts  7.53 us (4%)
    all_to_all x1, waiting for transfers between devices, lax.all_to_all(jnp.stack(jnp.split(q_in, lax.axis_size(axis_tag), axis=ar...  76.1 us
    all_to_all x1, blocking collectives, copy_for_each(): lax.all_to_all(jnp.broadcast_to(x[None], (count, *x.shape)), axis, 0, 0,...  46.8 us
    all_to_all x2, starting transfers between devices, copy_for_each(): lax.all_to_all(jnp.broadcast_to(x[None], (count, *x.shape)), axis, 0, 0,...  17.8 us
    reduce_sum x1, other arithmetic, per_device(): total_down = over_copies(jnp.sum(jnp.abs(fresh_down), axis=2), 'rows')  5.6 us
    all_to_all x1, starting transfers between devices, lax.all_to_all(jnp.stack(jnp.split(q_in, lax.axis_size(axis_tag), axis=ar...  5.01 us
    convert_element_type x1, other arithmetic, per_device(): (fresh_down / jnp.expand_dims(scale_down, 2)).astype(jnp.bfloat16)  4.74 us
  transfers between devices with their start and end apart: 3, of which 2 were waited for; matrix products, arithmetic and copies ran while one was open for 8% of the time, Pallas kernels for 0%

profile of v1, /device:TPU:9, one launch (start us, length us, event | category | flops | bytes accessed | tf_op | source)
XLA Modules:
  0.0 169.1 jit_solution(14877156339228353876)
XLA Ops:
  0.6 0.7 multiply_convert_fusion
  1.3 0.6 broadcast_in_dim.9
  1.9 11.1 %all-to-all-start.2 = ((bf16[32,128,2]{1,2,0:T(2,128)(2,1)}), bf16[32,128,2]{1,2,0:T(2,128)(2,1)S(1)}, u32[]{:S(2)}, u32[]{:S(2)}) async-start(bf16[32,128,2]{1,2,0:T(2,128)(2,1)} %broadcast_in_dim.9), calls=%async_computation.2 | async-start | bytes 32768 | tf_op jit(solution)/shard_map/all_to_all | solution.py:20
  13.1 5.6 %abs_reduce_fusion = f32[2,6400]{1,0:T(2,128)S(1)} fusion(f32[2,6400,128]{2,1,0:T(8,128)} %param.4, bf16[2,6400,128]{2,1,0:T(8,128)(2,1)} %param.5), kind=kLoop, calls=%fused_computation.1 | loop fusion | flops 6540800 | bytes 9881600 | tf_op jit(solution)/shard_map/reduce_sum | solution.py:40
  18.7 0.0 copy-start
  18.7 2.0 %all-to-all-done.2 = bf16[32,128,2]{1,2,0:T(2,128)(2,1)S(1)} async-done(((bf16[32,128,2]{1,2,0:T(2,128)(2,1)}), bf16[32,128,2]{1,2,0:T(2,128)(2,1)S(1)}, u32[]{:S(2)}, u32[]{:S(2)}) %all-to-all-start.2) | async-done | bytes 16416 | tf_op jit(solution)/shard_map/all_to_all | solution.py:20
  20.7 0.4 broadcast_in_dim.8
  21.1 46.8 %all_to_all.20 = f32[32,2,6400]{2,1,0:T(2,128)} all-to-all(f32[32,2,6400]{2,1,0:T(2,128)S(1)} %broadcast_in_dim.8), channel_id=1, replica_groups=mesh['owner'=8,'rows'=32] {'rows'}, dimensions={0} | all-to-all | bytes 3276800 | tf_op jit(solution)/shard_map/all_to_all | solution.py:20
  67.9 0.7 broadcast_in_dim.11
  68.6 6.7 %all-to-all-start.3 = ((bf16[8,4096,2]{1,2,0:T(2,128)(2,1)}), bf16[8,4096,2]{1,2,0:T(2,128)(2,1)S(1)}, u32[]{:S(2)}, u32[]{:S(2)}) async-start(bf16[8,4096,2]{1,2,0:T(2,128)(2,1)} %broadcast_in_dim.11), calls=%async_computation.3 | async-start | bytes 262144 | tf_op jit(solution)/shard_map/all_to_all | solution.py:20
  75.4 1.9 %reduce_sum.19 = f32[2,6400]{1,0:T(2,128)S(1)} reduce(f32[32,2,6400]{2,1,0:T(2,128)} %all_to_all.20, f32[]{:T(128)} %constant.6.clone.1), dimensions={0}, to_apply=%region_1.0 | reduce | flops 396800 | bytes 1689604 | tf_op jit(solution)/shard_map/reduce_sum | solution.py:25
  77.3 0.0 copy-done
  77.3 4.7 %divide_convert_fusion = bf16[2,6400,128]{2,1,0:T(8,128)(2,1)S(1)} fusion(f32[2,6400,128]{2,1,0:T(8,128)} %param.4, bf16[2,6400,128]{2,1,0:T(8,128)(2,1)S(1)} %copy-done, f32[2,6400]{1,0:T(2,128)S(1)} %broadcast_multiply_fusion), kind=kLoop, calls=%fused_computation | loop fusion | flops 6553600 | bytes 13158400 | tf_op jit(solution)/shard_map/convert_element_type | solution.py:42
  82.8 0.0 copy-start.1
  82.8 1.7 %copy-done.1 = bf16[32,2,200,128]{3,2,1,0:T(8,128)(2,1)} copy-done((bf16[32,2,200,128]{3,2,1,0:T(8,128)(2,1)}, bf16[32,2,200,128]{3,2,1,0:T(8,128)(2,1)S(1)}, u32[]{:S(2)}) %copy-start.1) | copy-done | bytes 3276824
  84.5 0.0 all-to-all-done.3
  84.5 5.0 %all-to-all-start.1 = ((bf16[32,2,200,128]{3,2,1,0:T(8,128)(2,1)}), bf16[32,2,200,128]{3,2,1,0:T(8,128)(2,1)S(1)}, u32[]{:S(2)}, u32[]{:S(2)}) async-start(bf16[32,2,200,128]{3,2,1,0:T(8,128)(2,1)} %copy-done.1), calls=%async_computation.1 | async-start | bytes 6553600 | tf_op jit(solution)/shard_map/all_to_all | solution.py:8
  89.5 0.7 reshape.24
  90.3 0.7 constant_dynamic-slice_fusion
  90.9 76.1 %all-to-all-done.1 = bf16[32,2,200,128]{3,2,1,0:T(8,128)(2,1)S(1)} async-done(((bf16[32,2,200,128]{3,2,1,0:T(8,128)(2,1)}), bf16[32,2,200,128]{3,2,1,0:T(8,128)(2,1)S(1)}, u32[]{:S(2)}, u32[]{:S(2)}) %all-to-all-start.1) | async-done | bytes 3276832 | tf_op jit(solution)/shard_map/all_to_all | solution.py:8
  167.0 2.1 %copy_bitcast_fusion = bf16[2,200,4096]{2,1,0:T(8,128)(2,1)} fusion(bf16[32,2,200,128]{3,2,1,0:T(8,128)(2,1)S(1)} %all-to-all-done.1), kind=kLoop, calls=%fused_computation.3 | loop fusion | bytes 6553600 | tf_op jit(solution)/shard_map/reshape | solution.py:7
  (33 shorter events, 0.6 us)
Async XLA Ops:
  1.9 18.8 %all-to-all-start.2 = ((bf16[32,128,2]{1,2,0:T(2,128)(2,1)}), bf16[32,128,2]{1,2,0:T(2,128)(2,1)S(1)}, u32[]{:S(2)}, u32[]{:S(2)}) async-start(bf16[32,128,2]{1,2,0:T(2,128)(2,1)} %broadcast_in_dim.9), calls=%async_computation.2 | async-start | bytes 32768 | tf_op jit(solution)/shard_map/all_to_all | solution.py:20
  18.7 58.6 %copy-start = (bf16[2,6400,128]{2,1,0:T(8,128)(2,1)S(1)}, bf16[2,6400,128]{2,1,0:T(8,128)(2,1)}, u32[]{:S(2)}) copy-start(bf16[2,6400,128]{2,1,0:T(8,128)(2,1)} %param.5) | copy-start | bytes 9830404
  68.6 15.9 %all-to-all-start.3 = ((bf16[8,4096,2]{1,2,0:T(2,128)(2,1)}), bf16[8,4096,2]{1,2,0:T(2,128)(2,1)S(1)}, u32[]{:S(2)}, u32[]{:S(2)}) async-start(bf16[8,4096,2]{1,2,0:T(2,128)(2,1)} %broadcast_in_dim.11), calls=%async_computation.3 | async-start | bytes 262144 | tf_op jit(solution)/shard_map/all_to_all | solution.py:20
  82.8 1.7 %copy-start.1 = (bf16[32,2,200,128]{3,2,1,0:T(8,128)(2,1)}, bf16[32,2,200,128]{3,2,1,0:T(8,128)(2,1)S(1)}, u32[]{:S(2)}) copy-start(bf16[32,2,200,128]{3,2,1,0:T(8,128)(2,1)S(1)} %fusion) | copy-start | bytes 9830404
  84.5 82.5 %all-to-all-start.1 = ((bf16[32,2,200,128]{3,2,1,0:T(8,128)(2,1)}), bf16[32,2,200,128]{3,2,1,0:T(8,128)(2,1)S(1)}, u32[]{:S(2)}, u32[]{:S(2)}) async-start(bf16[32,2,200,128]{3,2,1,0:T(8,128)(2,1)} %copy-done.1), calls=%async_computation.1 | async-start | bytes 6553600 | tf_op jit(solution)/shard_map/all_to_all | solution.py:8
